TPU v7x, 32 devices: a whole 2x2x4 slice. The times are simulated.
32 devices in a mesh: expert: 4 (over y, x), tensor: 4 (over z), rep: 2 (over core).
Axes of the slice: x: 2, y: 2, z: 4, core: 2. Of those that a mesh axis runs over, the one named last changes fastest.
Arguments:
- requests: bfloat16 [512, 1536], P('expert', ('tensor', 'rep')), may hold values from -6 to 6
- expert_ids: int32 [512, 2], P('expert'), may hold values from 0 to 3, all different within a row; in each aligned block of 128 rows (0 to 127, 128 to 255, ...) at most 96 rows name the same one
- gate_values: float32 [512, 2], P('expert'), may hold values from 0.2 to 1
- w_up: bfloat16 [4, 1536, 6144], P(None, 'expert', ('tensor', 'rep')), may hold values from -0.15625 to 0.15625
- w_down: bfloat16 [4, 1536, 6144], P(None, 'expert', ('tensor', 'rep')), may hold values from -0.078125 to 0.078125
- tower_in: bfloat16 [1536, 768], P(('tensor', 'rep')), may hold values from -0.15625 to 0.15625
- tower_bias: float32 [768], replicated, may hold values from -3 to 3
- tower_out: float32 [3, 256], replicated, may hold values from -0.375 to 0.375
- out_bias: float32 [3], replicated, may hold values from -3 to 3
Outputs:
- mixed: bfloat16 [512, 1536], P('expert', ('tensor', 'rep'))
- scores: float32 [3, 512], P(None, ('expert', 'tensor', 'rep'))
Inputs may be any that keep to these rules, and one draw needn't show every extreme that they name: `expert_ids`: each row names two different experts. In the rows of one device (128 requests) no expert is named more than 96 times, a bound that some block reaches.
All inputs are finite; a program needn't handle non-finite values.
Results may differ from a plain program's by a relative error of at most 0.015.
Values may be sent and summed in bfloat16 or wider, within the bound.
No kernel may reach another device: no remote copies, remote signals or barrier semaphores. Data moves between devices by JAX's collectives and lax.ppermute only.
A program may use at most 64 MiB of HBM per device.

v0:
```python
import jax
import jax.numpy as jnp
from jax import lax
from jax.sharding import PartitionSpec as P


def tower_head(pre, tower_bias, tower_out, out_bias):
    active = jax.nn.relu(pre + tower_bias[None, :])
    active = active.reshape(pre.shape[0], tower_out.shape[0], tower_out.shape[1])
    logits = jnp.sum(active * tower_out[None, :, :], axis=2) + out_bias[None, :]
    return jax.nn.sigmoid(logits).T


def per_device(
    requests, expert_ids, gate_values, w_up, w_down, tower_in, tower_bias, tower_out, out_bias
):
    groups = lax.axis_size("expert")
    experts = w_up.shape[0]
    local_experts = experts // groups
    tok_rows = requests.shape[0]
    capacity = 3 * tok_rows // experts
    serve_up, serve_down = (
        lax.all_to_all(w_up, "expert", split_axis=0, concat_axis=1, tiled=True),
        lax.all_to_all(w_down, "expert", split_axis=0, concat_axis=1, tiled=True),
    )
    flat_ids = expert_ids.reshape(-1)
    onehot = (flat_ids[:, None] == jnp.arange(experts, dtype=jnp.int32)[None, :]).astype(jnp.int32)
    before = jnp.cumsum(onehot, axis=0) - onehot
    slot_rank = jnp.sum(before * onehot, axis=1)
    slots = (flat_ids * capacity + slot_rank).reshape(tok_rows, 2)
    slot_index = jnp.arange(experts * capacity, dtype=jnp.int32)
    spread = (
        (slot_index[:, None] == slots[None, :, 0]) | (slot_index[:, None] == slots[None, :, 1])
    ).astype(jnp.bfloat16)
    full_rows = lax.all_gather(requests, ("tensor", "rep"), axis=1, tiled=True)
    outgoing = jnp.dot(spread, full_rows, preferred_element_type=jnp.float32).astype(jnp.bfloat16)
    incoming = lax.all_to_all(outgoing, "expert", split_axis=0, concat_axis=0, tiled=True)
    shaped = incoming.reshape(groups, local_experts, capacity, incoming.shape[1])
    hidden_pre = jnp.einsum("secd,edh->sech", shaped, serve_up, preferred_element_type=jnp.float32)
    hidden = jax.nn.relu(hidden_pre).astype(jnp.bfloat16)
    partial_value = jnp.einsum(
        "sech,edh->secd", hidden, serve_down, preferred_element_type=jnp.float32
    )
    summed = lax.psum_scatter(
        partial_value.astype(jnp.bfloat16), ("tensor", "rep"), scatter_dimension=3, tiled=True
    ).astype(jnp.float32)
    expert_out = summed.astype(jnp.bfloat16).reshape(
        groups * local_experts * capacity, summed.shape[3]
    )
    returned = lax.all_to_all(expert_out, "expert", split_axis=0, concat_axis=0, tiled=True)
    pick_first = (slots[:, 0:1] == slot_index[None, :]).astype(jnp.bfloat16)
    pick_second = (slots[:, 1:2] == slot_index[None, :]).astype(jnp.bfloat16)
    first = jnp.dot(pick_first, returned, preferred_element_type=jnp.float32)
    second = jnp.dot(pick_second, returned, preferred_element_type=jnp.float32)
    mixed = (gate_values[:, 0:1] * first + gate_values[:, 1:2] * second).astype(jnp.bfloat16)
    pre = lax.psum_scatter(
        jnp.dot(mixed, tower_in, preferred_element_type=jnp.float32).astype(jnp.bfloat16),
        ("tensor", "rep"),
        scatter_dimension=0,
        tiled=True,
    ).astype(jnp.float32)
    scores = tower_head(pre, tower_bias, tower_out, out_bias)
    return (mixed, scores)


def solution(mesh):
    in_specs = (
        P("expert", ("tensor", "rep")),
        P("expert", None),
        P("expert", None),
        P(None, "expert", ("tensor", "rep")),
        P(None, "expert", ("tensor", "rep")),
        P(("tensor", "rep"), None),
        P(),
        P(),
        P(),
    )
    out_specs = (P("expert", ("tensor", "rep")), P(None, ("expert", "tensor", "rep")))
    return jax.shard_map(
        per_device, mesh=mesh, in_specs=in_specs, out_specs=out_specs, check_vma=False
    )
```

profile of v0, /device:TPU:0, one launch (start us, length us, event | category | flops | bytes accessed | tf_op | source)
XLA Modules:
  0.0 198.6 jit_solution(8744839714044765721)
XLA Ops:
  7.2 0.0 copy-start
  7.2 0.0 reduce-scatter.7.cloned.1.call-start
  7.2 0.8 copy.32
  8.0 0.1 eq.85
  8.2 0.1 eq.81
  8.3 1.2 reduce-window.6
  9.6 0.1 slice.26
  9.6 0.1 copy.34
  9.8 0.1 copy.35
  9.9 0.1 add_bitcast_fusion
  10.0 0.1 reduce_sum.21
  10.1 0.1 copy.36
  10.2 0.7 multiply_add_fusion
  10.9 16.4 %all_gather.3 = bf16[128,1536]{0,1:T(8,128)(2,1)S(1)} all-gather(bf16[128,192]{0,1:T(8,128)(2,1)} %param.9), channel_id=1, replica_groups=mesh['expert'=4,'tensor'=4,'rep'=2] {'tensor','rep'}, dimensions={1}, use_global_device_ids=true | all-gather | bytes 442368 | tf_op jit(solution)/shard_map/all_gather | solution.py:35
  27.3 0.5 convolution_convert_fusion
  27.8 0.0 copy-start.1
  27.8 19.8 %all_to_all.39 = bf16[4,96,1536]{2,1,0:T(8,128)(2,1)} all-to-all(bf16[4,96,1536]{2,1,0:T(8,128)(2,1)S(1)} %bitcast.56), channel_id=1, replica_groups=mesh['expert'=4,'tensor'=4,'rep'=2] {'expert'}, dimensions={0} | all-to-all | bytes 2359296 | tf_op jit(solution)/shard_map/all_to_all | solution.py:37
  47.6 0.0 copy-done.1
  47.6 30.1 %all_to_all.40 = bf16[4,384,768]{2,1,0:T(8,128)(2,1)S(1)} all-to-all(bf16[4,384,768]{2,1,0:T(8,128)(2,1)S(1)} %copy-done.1), channel_id=1, replica_groups=mesh['expert'=4,'tensor'=4,'rep'=2] {'expert'}, dimensions={0} | all-to-all | bytes 4718592 | tf_op jit(solution)/shard_map/all_to_all | solution.py:23
  77.7 0.0 copy-done.2
  77.7 29.5 %all_to_all.41 = bf16[4,384,768]{2,1,0:T(8,128)(2,1)} all-to-all(bf16[4,384,768]{2,1,0:T(8,128)(2,1)S(1)} %copy-done.2), channel_id=1, replica_groups=mesh['expert'=4,'tensor'=4,'rep'=2] {'expert'}, dimensions={0} | all-to-all | bytes 4718592 | tf_op jit(solution)/shard_map/all_to_all | solution.py:24
  107.3 5.5 %fusion = bf16[4,1,96,1536]{3,2,0,1:T(8,128)(2,1)} fusion(bf16[1536,768,1]{1,0,2:T(8,128)(2,1)} %bitcast.58, bf16[4,96,1536]{2,1,0:T(8,128)(2,1)} %all_to_all.39, bf16[1536,768,1]{1,0,2:T(8,128)(2,1)S(1)} %bitcast.57), kind=kOutput, calls=%fused_computation.2 | convolution fusion | flops 1813118976 | bytes 7077888 | tf_op jit(solution)/shard_map/sech,edh->secd/dot_general | solution.py:41
  112.7 2.6 %copy.38 = bf16[4,1,96,1536]{2,0,1,3:T(4,128)(2,1)S(1)} copy(bf16[4,1,96,1536]{3,2,0,1:T(8,128)(2,1)} %fusion) | data formatting | bytes 2359296
  115.4 1.9 reshape.69
  117.3 0.0 reduce-scatter.7.cloned.1.call-update
  117.3 0.0 copy-start.5
  117.3 0.0 copy-start.7
  117.3 32.7 %reduce-scatter.7.cloned.1.call-done = bf16[192,384]{1,0:T(8,128)(2,1)} async-done(((bf16[1536,384]{1,0:T(8,128)(2,1)}), bf16[192,384]{1,0:T(8,128)(2,1)}) %reduce-scatter.7.cloned.1.call-update) | async-done | bytes 147472
  150.0 1.1 reshape.70
  151.0 0.8 copy.39
  151.9 3.6 %all-to-all-start.3 = ((bf16[4,96,192]{2,1,0:T(8,128)(2,1)}), bf16[4,96,192]{2,1,0:T(8,128)(2,1)S(1)}, u32[]{:S(2)}, u32[]{:S(2)}) async-start(bf16[4,96,192]{2,1,0:T(8,128)(2,1)} %bitcast.13), calls=%async_computation.3 | async-start | bytes 393216 | tf_op jit(solution)/shard_map/all_to_all | solution.py:50
  155.5 0.0 reduce-scatter.5.cloned.1.call-start
  155.5 0.0 copy-done.6
  155.5 5.2 %all-to-all-done.3 = bf16[4,96,192]{2,1,0:T(8,128)(2,1)S(1)} async-done(((bf16[4,96,192]{2,1,0:T(8,128)(2,1)}), bf16[4,96,192]{2,1,0:T(8,128)(2,1)S(1)}, u32[]{:S(2)}, u32[]{:S(2)}) %all-to-all-start.3) | async-done | bytes 147488 | tf_op jit(solution)/shard_map/all_to_all | solution.py:50
  160.7 0.3 convolution_multiply_fusion
  161.0 0.3 fusion.3
  161.3 0.0 copy-done
  161.3 0.0 copy-start.3
  161.3 0.9 convolution_convert_fusion.2
  162.2 0.0 reduce-scatter.5.cloned.1.call-update
  162.2 27.9 %reduce-scatter.5.cloned.1.call-done = bf16[16,768]{1,0:T(8,128)(2,1)} async-done(((bf16[128,768]{1,0:T(8,128)(2,1)}), bf16[16,768]{1,0:T(8,128)(2,1)}) %reduce-scatter.5.cloned.1.call-update) | async-done | bytes 24592 | tf_op jit(solution)/shard_map/reduce_scatter | solution.py:56
  190.2 0.0 copy-done.4
  190.2 0.7 add_maximum_fusion
  190.9 0.0 copy-done.5
  191.0 0.1 multiply_reduce_fusion
  191.1 0.0 copy-done.7
  191.1 0.7 copy.37
  191.7 0.0 copy-done.3
  (11 shorter events, 0.1 us)
Async XLA Ops:
  7.2 154.1 %copy-start = (bf16[192,768]{1,0:T(8,128)(2,1)S(1)}, bf16[192,768]{1,0:T(8,128)(2,1)}, u32[]{:S(2)}) copy-start(bf16[192,768]{1,0:T(8,128)(2,1)} %param.14) | copy-start | bytes 884740
  7.2 142.8 %reduce-scatter.7.cloned.1.call-start = ((), (), s32[]{:S(2)}) async-start(), calls=%async_computation.7 | async-start | bytes 1327104
  27.8 19.8 %copy-start.1 = (bf16[4,384,768]{2,1,0:T(8,128)(2,1)S(1)}, bf16[4,384,768]{2,1,0:T(8,128)(2,1)}, u32[]{:S(2)}) copy-start(bf16[4,384,768]{2,1,0:T(8,128)(2,1)} %param.12) | copy-start | bytes 7077892
  47.6 30.1 %copy-start.2 = (bf16[4,384,768]{2,1,0:T(8,128)(2,1)S(1)}, bf16[4,384,768]{2,1,0:T(8,128)(2,1)}, u32[]{:S(2)}) copy-start(bf16[4,384,768]{2,1,0:T(8,128)(2,1)} %param.13) | copy-start | bytes 7077892
  117.3 38.2 %copy-start.6 = (f32[128,2]{0,1:T(2,128)S(1)}, f32[128,2]{0,1:T(2,128)}, u32[]{:S(2)}) copy-start(f32[128,2]{0,1:T(2,128)} %param.11) | copy-start | bytes 3076
  117.3 72.9 %copy-start.4 = (f32[768]{0:T(1024)S(1)}, f32[768]{0:T(1024)}, u32[]{:S(2)}) copy-start(f32[768]{0:T(1024)} %param.15) | copy-start | bytes 9220
  117.3 73.7 %copy-start.5 = (f32[3,256]{1,0:T(4,128)S(1)}, f32[3,256]{1,0:T(4,128)}, u32[]{:S(2)}) copy-start(f32[3,256]{1,0:T(4,128)} %param.16) | copy-start | bytes 9220
  117.3 73.7 %copy-start.7 = (f32[3]{0:T(128)S(1)}, f32[3]{0:T(128)}, u32[]{:S(2)}) copy-start(f32[3]{0:T(128)} %param.17) | copy-start | bytes 40
  151.9 8.8 %all-to-all-start.3 = ((bf16[4,96,192]{2,1,0:T(8,128)(2,1)}), bf16[4,96,192]{2,1,0:T(8,128)(2,1)S(1)}, u32[]{:S(2)}, u32[]{:S(2)}) async-start(bf16[4,96,192]{2,1,0:T(8,128)(2,1)} %bitcast.13), calls=%async_computation.3 | async-start | bytes 393216 | tf_op jit(solution)/shard_map/all_to_all | solution.py:50
  155.5 34.7 %reduce-scatter.5.cloned.1.call-start = ((), (), s32[]{:S(2)}) async-start(), calls=%async_computation.6 | async-start | bytes 221184 | tf_op jit(solution)/shard_map/reduce_scatter | solution.py:56
  161.3 30.5 %copy-start.3 = (bf16[128,192]{0,1:T(8,128)(2,1)}, bf16[128,192]{0,1:T(8,128)(2,1)S(1)}, u32[]{:S(2)}) copy-start(bf16[128,192]{0,1:T(8,128)(2,1)S(1)} %fusion.3) | copy-start | bytes 147460
Sparse Core Ops, SparseCore 0:
  117.4 32.5 reduce-scatter.6
  162.4 27.7 reduce-scatter.4
where the time goes:
time: 199 us
  blocking collectives  95.8 us (48%)
  waiting for transfers between devices  65.8 us (33%)
  between operations  14.2 us (7%)
  local copies, waits for them, and re-layouts  8.73 us (4%)
  matrix products  7.42 us (4%)
  starting transfers between devices  3.68 us (2%)
  other arithmetic  2.92 us (1%)
    unnamed x3, waiting for transfers between devices  32.7 us
    all_to_all x1, blocking collectives, per_device(): lax.all_to_all(w_up, 'expert', split_axis=0, concat_axis=1, tiled=True)  30.1 us
    all_to_all x1, blocking collectives, per_device(): lax.all_to_all(w_down, 'expert', split_axis=0, concat_axis=1, tiled=True)  29.5 us
    reduce_scatter x1, waiting for transfers between devices, per_device(): lax.psum_scatter(jnp.dot(mixed, tower_in, preferred_element_type=jnp.floa...  27.9 us
    all_to_all x1, blocking collectives, per_device(): lax.all_to_all(outgoing, 'expert', split_axis=0, concat_axis=0, tiled=True)  19.8 us
    all_gather x1, blocking collectives, per_device(): full_rows = lax.all_gather(requests, ('tensor', 'rep'), axis=1, tiled=True)  16.4 us
    unnamed x22, local copies, waits for them, and re-layouts  7.94 us
    dot_general x1, matrix products, per_device(): jnp.einsum('sech,edh->secd', hidden, serve_down, preferred_element_type=j...  5.47 us
  transfers between devices with their start and end apart: 3, of which 3 were waited for; matrix products, arithmetic and copies ran while one was open for 0% of the time, Pallas kernels for 0%

commit v1 on v0

--- a/solution.py
+++ b/solution.py
@@ -34,7 +34,15 @@
     ).astype(jnp.bfloat16)
     full_rows = lax.all_gather(requests, ("tensor", "rep"), axis=1, tiled=True)
     outgoing = jnp.dot(spread, full_rows, preferred_element_type=jnp.float32).astype(jnp.bfloat16)
-    incoming = lax.all_to_all(outgoing, "expert", split_axis=0, concat_axis=0, tiled=True)
+    ways, here = (lax.axis_size("expert"), lax.axis_index("expert"))
+    width = outgoing.shape[0] // ways
+    turned = jnp.roll(outgoing, -here * width, axis=0)
+    got = [lax.slice_in_dim(turned, 0, width, axis=0)]
+    for far in range(1, ways):
+        sent = lax.slice_in_dim(turned, far * width, (far + 1) * width, axis=0)
+        got.append(lax.ppermute(sent, "expert", [(d, (d + far) % ways) for d in range(ways)]))
+    line = jnp.concatenate(got[::-1], axis=0)
+    incoming = jnp.roll(line, (here + 1) * got[0].shape[0], axis=0)
     shaped = incoming.reshape(groups, local_experts, capacity, incoming.shape[1])
     hidden_pre = jnp.einsum("secd,edh->sech", shaped, serve_up, preferred_element_type=jnp.float32)
     hidden = jax.nn.relu(hidden_pre).astype(jnp.bfloat16)

time: 199 us -> 184 us (0.925)
  blocking collectives: 95.8 us -> 15 us
  waiting for transfers between devices: 65.8 us -> 110 us
  starting transfers between devices: 3.68 us -> 17.5 us
  other arithmetic: 2.92 us -> 9.93 us
    all_to_all x3 -> x0, blocking collectives: 79.4 us -> none  [the longest x1 30.1 us: per_device(): lax.all_to_all(w_up, 'expert', split_axis=0, concat_axis=1, tiled=True)]
    all_to_all x0 -> x2, waiting for transfers between devices: none -> 25.4 us  [the longest x1 25.4 us: per_device(): lax.all_to_all(w_up, 'expert', split_axis=0, concat_axis=1, tiled=True)]
    ppermute x0 -> x3, waiting for transfers between devices: none -> 19 us  [per_device(): lax.ppermute(sent, 'expert', [(d, (d + far) % ways) for d in range(ways)])]
    all_to_all x0 -> x2, starting transfers between devices: none -> 9.84 us  [the longest x1 5.34 us: per_device(): lax.all_to_all(w_up, 'expert', split_axis=0, concat_axis=1, tiled=True)]
    concatenate x0 -> x2, other arithmetic: none -> 7.7 us  [the longest x1 6.23 us: per_device(): incoming = jnp.roll(line, (here + 1) * got[0].shape[0], axis=0)]
    ppermute x0 -> x3, starting transfers between devices: none -> 3.91 us  [per_device(): lax.ppermute(sent, 'expert', [(d, (d + far) % ways) for d in range(ways)])]
  transfers between devices with their start and end apart: 3 -> 8, of which waited for: 3 -> 6; matrix products, arithmetic and copies ran while one was open for 0% -> 6% of each run, Pallas kernels for 0% -> 0%
where the time goes in v1:
time: 184 us; the launch traced here: 183 us
  waiting for transfers between devices  110 us (60%)
  starting transfers between devices  17.5 us (10%)
  blocking collectives  15 us (8%)
  between operations  14.2 us (8%)
  other arithmetic  9.93 us (5%)
  local copies, waits for them, and re-layouts  8.92 us (5%)
  matrix products  7.45 us (4%)
    unnamed x3, waiting for transfers between devices  32.7 us
    reduce_scatter x1, waiting for transfers between devices, per_device(): lax.psum_scatter(jnp.dot(mixed, tower_in, preferred_element_type=jnp.floa...  27.8 us
    all_to_all x1, waiting for transfers between devices, per_device(): lax.all_to_all(w_up, 'expert', split_axis=0, concat_axis=1, tiled=True)  25.4 us
    ppermute x3, waiting for transfers between devices, per_device(): lax.ppermute(sent, 'expert', [(d, (d + far) % ways) for d in range(ways)])  19 us
    all_gather x1, blocking collectives, per_device(): full_rows = lax.all_gather(requests, ('tensor', 'rep'), axis=1, tiled=True)  15 us
    unnamed x22, local copies, waits for them, and re-layouts  7.22 us
    concatenate x1, other arithmetic, per_device(): incoming = jnp.roll(line, (here + 1) * got[0].shape[0], axis=0)  6.23 us
    dot_general x1, matrix products, per_device(): jnp.einsum('sech,edh->secd', hidden, serve_down, preferred_element_type=j...  5.5 us
  transfers between devices with their start and end apart: 8, of which 6 were waited for; matrix products, arithmetic and copies ran while one was open for 6% of the time, Pallas kernels for 0%

profile of v1, /device:TPU:0, one launch (start us, length us, event | category | flops | bytes accessed | tf_op | source)
XLA Modules:
  0.0 183.1 jit_solution(1103523423884069744)
XLA Ops:
  7.2 0.0 copy-start
  7.2 5.3 %all-to-all-start = ((bf16[4,384,768]{2,1,0:T(8,128)(2,1)}), bf16[4,384,768]{2,1,0:T(8,128)(2,1)S(1)}, u32[]{:S(2)}, u32[]{:S(2)}) async-start(bf16[4,384,768]{2,1,0:T(8,128)(2,1)} %param.14), calls=%async_computation | async-start | bytes 4718592 | tf_op jit(solution)/shard_map/all_to_all | solution.py:23
  12.5 0.0 copy-done.3
  12.5 0.1 copy.32
  12.6 0.1 eq.87
  12.8 0.1 eq.83
  12.9 1.2 reduce-window.6
  14.2 0.1 slice.42
  14.2 0.1 copy.34
  14.4 0.1 copy.35
  14.5 0.1 add_bitcast_fusion
  14.6 0.1 reduce_sum.21
  14.7 0.1 copy.36
  14.8 0.0 copy-start.2
  14.8 25.4 %all-to-all-done = bf16[4,384,768]{2,1,0:T(8,128)(2,1)S(1)} async-done(((bf16[4,384,768]{2,1,0:T(8,128)(2,1)}), bf16[4,384,768]{2,1,0:T(8,128)(2,1)S(1)}, u32[]{:S(2)}, u32[]{:S(2)}) %all-to-all-start) | async-done | bytes 2359328 | tf_op jit(solution)/shard_map/all_to_all | solution.py:23
  40.2 4.5 %all-to-all-start.1 = ((bf16[4,384,768]{2,1,0:T(8,128)(2,1)}), bf16[4,384,768]{2,1,0:T(8,128)(2,1)}, u32[]{:S(2)}, u32[]{:S(2)}) async-start(bf16[4,384,768]{2,1,0:T(8,128)(2,1)} %param.15), calls=%async_computation.1 | async-start | bytes 4718592 | tf_op jit(solution)/shard_map/all_to_all | solution.py:24
  44.7 0.0 reduce-scatter.7.cloned.1.call-start
  44.8 15.0 %all_gather.3 = bf16[128,1536]{0,1:T(8,128)(2,1)S(1)} all-gather(bf16[128,192]{0,1:T(8,128)(2,1)S(1)} %copy-done.2), channel_id=1, replica_groups=mesh['expert'=4,'tensor'=4,'rep'=2] {'tensor','rep'}, dimensions={1}, use_global_device_ids=true | all-gather | bytes 442368 | tf_op jit(solution)/shard_map/all_gather | solution.py:35
  59.7 0.5 convolution_convert_fusion
  60.2 1.5 fusion.9
  61.7 0.9 fusion.23
  62.6 2.8 %collective-permute-start = (bf16[96,1536]{1,0:T(8,128)(2,1)}, bf16[96,1536]{1,0:T(8,128)(2,1)S(1)}, u32[]{:S(2)}, u32[]{:S(2)}) collective-permute-start(bf16[96,1536]{1,0:T(8,128)(2,1)} %get-tuple-element.10), channel_id=1, source_target_pairs={{0,24},{8,0},{16,8},{24,16},{1,25},{9,1},{17,9},{25,17},{2,26},{10... | collective-permute-start | bytes 884744 | tf_op jit(solution)/shard_map/ppermute | solution.py:43
  65.4 0.6 collective-permute-start.1
  65.9 0.6 collective-permute-start.2
  66.5 13.5 %collective-permute-done = bf16[96,1536]{1,0:T(8,128)(2,1)S(1)} collective-permute-done((bf16[96,1536]{1,0:T(8,128)(2,1)}, bf16[96,1536]{1,0:T(8,128)(2,1)S(1)}, u32[]{:S(2)}, u32[]{:S(2)}) %collective-permute-start) | collective-permute-done | bytes 294944 | tf_op jit(solution)/shard_map/ppermute | solution.py:43
  80.0 0.0 collective-permute-done.1
  80.0 5.5 %collective-permute-done.2 = bf16[96,1536]{1,0:T(8,128)(2,1)} collective-permute-done((bf16[96,1536]{1,0:T(8,128)(2,1)S(1)}, bf16[96,1536]{1,0:T(8,128)(2,1)}, u32[]{:S(2)}, u32[]{:S(2)}) %collective-permute-start.2) | collective-permute-done | bytes 294944 | tf_op jit(solution)/shard_map/ppermute | solution.py:43
  85.5 6.2 %fusion.5 = bf16[384,1536]{1,0:T(8,128)(2,1)} fusion(s32[]{:T(128)S(6)} %select_n.15, bf16[96,1536]{1,0:T(8,128)(2,1)S(1)} %collective-permute-done, bf16[96,1536]{1,0:T(8,128)(2,1)} %collective-permute-done.1, bf16[96,1536]{1,0:T(8,128)(2,1)} %collective-permute-done.2, bf16[96,1536]{1,0:T(8,128)(2,1)S(1)} %get-tuple-element.7), kind=kLoop, calls=%fused_computation.18 | loop fusion | flops 9437184 | bytes 2359300 | tf_op jit(solution)/shard_map/jit(_roll_dynamic)/concatenate | solution.py:45
  91.7 0.0 all-to-all-done.1
  91.7 5.5 %fusion = bf16[4,1,96,1536]{3,2,0,1:T(8,128)(2,1)} fusion(bf16[1536,768,1]{1,0,2:T(8,128)(2,1)} %bitcast.9, bf16[4,96,1536]{2,1,0:T(8,128)(2,1)} %bitcast.59, bf16[1536,768,1]{1,0,2:T(8,128)(2,1)S(1)} %bitcast.56), kind=kOutput, calls=%fused_computation.2 | convolution fusion | flops 1813118976 | bytes 7077888 | tf_op jit(solution)/shard_map/sech,edh->secd/dot_general | solution.py:49
  97.3 2.6 %copy.38 = bf16[4,1,96,1536]{2,0,1,3:T(4,128)(2,1)S(1)} copy(bf16[4,1,96,1536]{3,2,0,1:T(8,128)(2,1)} %fusion) | data formatting | bytes 2359296
  99.9 0.0 copy-start.6
  99.9 1.9 %reshape.69 = bf16[1536,384]{1,0:T(8,128)(2,1)} reshape(bf16[1536,1,4,96]{3,2,1,0:T(4,128)(2,1)S(1)} %bitcast.55) | data formatting | bytes 2359296
  101.8 0.0 reduce-scatter.7.cloned.1.call-update
  101.8 32.7 %reduce-scatter.7.cloned.1.call-done = bf16[192,384]{1,0:T(8,128)(2,1)} async-done(((bf16[1536,384]{1,0:T(8,128)(2,1)}), bf16[192,384]{1,0:T(8,128)(2,1)}) %reduce-scatter.7.cloned.1.call-update) | async-done | bytes 147472
  134.5 1.1 reshape.70
  135.5 0.8 copy.39
  136.4 3.7 %all-to-all-start.2 = ((bf16[4,96,192]{2,1,0:T(8,128)(2,1)}), bf16[4,96,192]{2,1,0:T(8,128)(2,1)S(1)}, u32[]{:S(2)}, u32[]{:S(2)}) async-start(bf16[4,96,192]{2,1,0:T(8,128)(2,1)} %bitcast.13), calls=%async_computation.2 | async-start | bytes 393216 | tf_op jit(solution)/shard_map/all_to_all | solution.py:58
  140.1 5.2 %all-to-all-done.2 = bf16[4,96,192]{2,1,0:T(8,128)(2,1)S(1)} async-done(((bf16[4,96,192]{2,1,0:T(8,128)(2,1)}), bf16[4,96,192]{2,1,0:T(8,128)(2,1)S(1)}, u32[]{:S(2)}, u32[]{:S(2)}) %all-to-all-start.2) | async-done | bytes 147488 | tf_op jit(solution)/shard_map/all_to_all | solution.py:58
  145.3 0.3 convolution_multiply_fusion
  145.6 0.3 fusion.11
  145.9 0.0 copy-start.1
  145.9 0.9 convolution_convert_fusion.2
  146.8 0.0 reduce-scatter.5.cloned.1.call-update
  146.8 27.8 %reduce-scatter.5.cloned.1.call-done = bf16[16,768]{1,0:T(8,128)(2,1)} async-done(((bf16[128,768]{1,0:T(8,128)(2,1)}), bf16[16,768]{1,0:T(8,128)(2,1)}) %reduce-scatter.5.cloned.1.call-update) | async-done | bytes 24592 | tf_op jit(solution)/shard_map/reduce_scatter | solution.py:64
  174.7 0.7 add_maximum_fusion
  175.5 0.1 multiply_reduce_fusion
  175.6 0.7 copy.37
  (21 shorter events, 0.2 us)
Async XLA Ops:
  7.2 138.7 %copy-start = (bf16[192,768]{1,0:T(8,128)(2,1)S(1)}, bf16[192,768]{1,0:T(8,128)(2,1)}, u32[]{:S(2)}) copy-start(bf16[192,768]{1,0:T(8,128)(2,1)} %param.16) | copy-start | bytes 884740
  7.2 5.3 %copy-start.3 = (s32[128,2]{0,1:T(2,128)S(1)}, s32[128,2]{0,1:T(2,128)}, u32[]{:S(2)}) copy-start(s32[128,2]{0,1:T(2,128)} %param.12) | copy-start | bytes 3076
  7.2 33.0 %all-to-all-start = ((bf16[4,384,768]{2,1,0:T(8,128)(2,1)}), bf16[4,384,768]{2,1,0:T(8,128)(2,1)S(1)}, u32[]{:S(2)}, u32[]{:S(2)}) async-start(bf16[4,384,768]{2,1,0:T(8,128)(2,1)} %param.14), calls=%async_computation | async-start | bytes 4718592 | tf_op jit(solution)/shard_map/all_to_all | solution.py:23
  14.8 30.0 %copy-start.2 = (bf16[128,192]{0,1:T(8,128)(2,1)S(1)}, bf16[128,192]{0,1:T(8,128)(2,1)}, u32[]{:S(2)}) copy-start(bf16[128,192]{0,1:T(8,128)(2,1)} %param.11) | copy-start | bytes 147460
  40.2 51.5 %all-to-all-start.1 = ((bf16[4,384,768]{2,1,0:T(8,128)(2,1)}), bf16[4,384,768]{2,1,0:T(8,128)(2,1)}, u32[]{:S(2)}, u32[]{:S(2)}) async-start(bf16[4,384,768]{2,1,0:T(8,128)(2,1)} %param.15), calls=%async_computation.1 | async-start | bytes 4718592 | tf_op jit(solution)/shard_map/all_to_all | solution.py:24
  44.7 89.8 %reduce-scatter.7.cloned.1.call-start = ((), (), s32[]{:S(2)}) async-start(), calls=%async_computation.6 | async-start | bytes 1327104
  62.6 17.4 %collective-permute-start = (bf16[96,1536]{1,0:T(8,128)(2,1)}, bf16[96,1536]{1,0:T(8,128)(2,1)S(1)}, u32[]{:S(2)}, u32[]{:S(2)}) collective-permute-start(bf16[96,1536]{1,0:T(8,128)(2,1)} %get-tuple-element.10), channel_id=1, source_target_pairs={{0,24},{8,0},{16,8},{24,16},{1,25},{9,1},{17,9},{25,17},{2,26},{10... | collective-permute-start | bytes 884744 | tf_op jit(solution)/shard_map/ppermute | solution.py:43
  65.4 14.6 %collective-permute-start.1 = (bf16[96,1536]{1,0:T(8,128)(2,1)}, bf16[96,1536]{1,0:T(8,128)(2,1)}, u32[]{:S(2)}, u32[]{:S(2)}) collective-permute-start(bf16[96,1536]{1,0:T(8,128)(2,1)} %get-tuple-element.9), channel_id=1, source_target_pairs={{0,16},{8,24},{16,0},{24,8},{1,17},{9,25},{17,1},{25,9},{2,18},{10... | collective-permute-start | bytes 884744 | tf_op jit(solution)/shard_map/ppermute | solution.py:43
  65.9 19.6 %collective-permute-start.2 = (bf16[96,1536]{1,0:T(8,128)(2,1)S(1)}, bf16[96,1536]{1,0:T(8,128)(2,1)}, u32[]{:S(2)}, u32[]{:S(2)}) collective-permute-start(bf16[96,1536]{1,0:T(8,128)(2,1)S(1)} %get-tuple-element.8), channel_id=1, source_target_pairs={{0,8},{8,16},{16,24},{24,0},{1,9},{9,17},{17,25},{25,1},{2,10},{10... | collective-permute-start | bytes 884744 | tf_op jit(solution)/shard_map/ppermute | solution.py:43
  99.9 40.2 %copy-start.6 = (f32[128,2]{0,1:T(2,128)S(1)}, f32[128,2]{0,1:T(2,128)}, u32[]{:S(2)}) copy-start(f32[128,2]{0,1:T(2,128)} %param.13) | copy-start | bytes 3076
  101.8 72.9 %copy-start.4 = (f32[768]{0:T(1024)S(1)}, f32[768]{0:T(1024)}, u32[]{:S(2)}) copy-start(f32[768]{0:T(1024)} %param.17) | copy-start | bytes 9220
  101.8 73.7 %copy-start.5 = (f32[3,256]{1,0:T(4,128)S(1)}, f32[3,256]{1,0:T(4,128)}, u32[]{:S(2)}) copy-start(f32[3,256]{1,0:T(4,128)} %param.18) | copy-start | bytes 9220
  101.8 73.8 %copy-start.7 = (f32[3]{0:T(128)S(1)}, f32[3]{0:T(128)}, u32[]{:S(2)}) copy-start(f32[3]{0:T(128)} %param.19) | copy-start | bytes 40
  136.4 8.9 %all-to-all-start.2 = ((bf16[4,96,192]{2,1,0:T(8,128)(2,1)}), bf16[4,96,192]{2,1,0:T(8,128)(2,1)S(1)}, u32[]{:S(2)}, u32[]{:S(2)}) async-start(bf16[4,96,192]{2,1,0:T(8,128)(2,1)} %bitcast.13), calls=%async_computation.2 | async-start | bytes 393216 | tf_op jit(solution)/shard_map/all_to_all | solution.py:58
  140.1 34.6 %reduce-scatter.5.cloned.1.call-start = ((), (), s32[]{:S(2)}) async-start(), calls=%async_computation.5 | async-start | bytes 221184 | tf_op jit(solution)/shard_map/reduce_scatter | solution.py:64
  145.9 30.4 %copy-start.1 = (bf16[128,192]{0,1:T(8,128)(2,1)}, bf16[128,192]{0,1:T(8,128)(2,1)S(1)}, u32[]{:S(2)}) copy-start(bf16[128,192]{0,1:T(8,128)(2,1)S(1)} %fusion.11) | copy-start | bytes 147460
Sparse Core Ops, SparseCore 0:
  101.9 32.4 reduce-scatter.6
  146.9 27.6 reduce-scatter.4
